TPU v7x, 32 devices: a whole 2x2x4 slice. The times are simulated.
32 devices in a mesh: section: 4 (over z), dp: 2 (over x), mp: 4 (over y, core).
Axes of the slice: x: 2, y: 2, z: 4, core: 2. Of those that a mesh axis runs over, the one named last changes fastest.
Arguments:
- entrance: bfloat16 [2, 2, 96, 4096], P('dp'), may hold values from -6 to 6
- lengths: int32 [2, 2], P('dp'), may hold values from 24 to 96
- positives: int32 [2], replicated, may hold values from 0 to 1, each once
- norm_gains: float32 [4, 4096], P('section'), may hold values from 0.5 to 1.5
- query_proj: bfloat16 [4, 4096, 2048], P('section', None, 'mp'), may hold values from -0.09375 to 0.09375
- key_proj: bfloat16 [4, 4096, 512], P('section', None, 'mp'), may hold values from -0.09375 to 0.09375
- value_proj: bfloat16 [4, 4096, 512], P('section', None, 'mp'), may hold values from -0.09375 to 0.09375
- out_proj: bfloat16 [4, 2048, 4096], P('section', 'mp'), may hold values from -0.125 to 0.125
Outputs:
- losses: float32 [4, 7], P('section')
- norm_gain_grad: float32 [4, 4096], P('section', ('dp', 'mp'))
- query_proj_grad: float32 [4, 4096, 2048], P('section', 'dp', 'mp')
- key_proj_grad: float32 [4, 4096, 512], P('section', 'dp', 'mp')
- value_proj_grad: float32 [4, 4096, 512], P('section', 'dp', 'mp')
- out_proj_grad: float32 [4, 2048, 4096], P('section', 'mp', 'dp')
Inputs may be any that keep to these rules, and one draw needn't show every extreme that they name: positives is a permutation of the pair indices. `lengths`: tokens at or past a sequence's length are padding.
All inputs are finite; a program needn't handle non-finite values.
Results may differ from a plain program's by a relative error of at most 0.039.
Values may be sent and summed in bfloat16 or wider, within the bound.
A program may use at most 128 MiB of HBM per device.

v0:
```python
import jax
import jax.numpy as jnp
from jax import lax
from jax.sharding import PartitionSpec as P

HEAD = 128
WIDTHS = 7
EPSILON = 1e-05
SOFTMAX_TEMPER = 0.05
ROPE_BASE = 500000.0


def passed_along(value, axis, steps):
    count = lax.axis_size(axis)
    first, last = (max(0, -steps), min(count, count - steps))
    return lax.ppermute(value, axis, [(source, source + steps) for source in range(first, last)])


def rope_tables(length, head_size):
    half_size = head_size // 2
    inverse_freq = ROPE_BASE ** (-jnp.arange(half_size, dtype=jnp.float32) * 2.0 / head_size)
    angles = jnp.arange(length, dtype=jnp.float32)[:, None] * inverse_freq[None, :]
    return (jnp.cos(angles), jnp.sin(angles))


def rotate(values, cosine, sine_table):
    half_size = values.shape[-1] // 2
    first_half = values[..., :half_size]
    second = values[..., half_size:]
    cosine = cosine[None, :, None, :]
    sine_table = sine_table[None, :, None, :]
    return jnp.concatenate(
        [first_half * cosine - second * sine_table, second * cosine + first_half * sine_table],
        axis=-1,
    )


def attend(query_pre, key_pre, value_pre):
    seq_count, length, query_width = query_pre.shape
    query_heads = query_width // HEAD
    kv_heads = key_pre.shape[-1] // HEAD
    group_size = query_heads // kv_heads
    cosine, sine_table = rope_tables(length, HEAD)
    query_vectors = rotate(
        query_pre.reshape(seq_count, length, query_heads, HEAD), cosine, sine_table
    ).astype(jnp.bfloat16)
    key_rows = rotate(
        key_pre.reshape(seq_count, length, kv_heads, HEAD), cosine, sine_table
    ).astype(jnp.bfloat16)
    values = value_pre.reshape(seq_count, length, kv_heads, HEAD).astype(jnp.bfloat16)
    query_vectors = query_vectors.reshape(seq_count, length, kv_heads, group_size, HEAD)
    scores = jnp.einsum(
        "sikge,sjke->skgij", query_vectors.astype(jnp.float32), key_rows.astype(jnp.float32)
    ) * HEAD ** (-0.5)
    causal = (
        jnp.arange(length, dtype=jnp.int32)[:, None] >= jnp.arange(length, dtype=jnp.int32)[None, :]
    )
    scores = jnp.where(causal, scores, -1e30)
    weights = jax.nn.softmax(scores, axis=-1).astype(jnp.bfloat16)
    mixture = jnp.einsum(
        "skgij,sjke->sikge", weights.astype(jnp.float32), values.astype(jnp.float32)
    )
    return mixture.reshape(seq_count, length, query_heads * HEAD)


def normalize(hidden_f, gain_vector):
    inv_rms = lax.rsqrt(jnp.mean(hidden_f * hidden_f, axis=-1, keepdims=True) + EPSILON)
    return hidden_f * inv_rms * gain_vector


def contract_rows(left, right):
    return lax.dot_general(
        left, right, (((0,), (0,)), ((), ())), preferred_element_type=jnp.float32
    )


def contract_last(left, right):
    return lax.dot_general(
        left, right, (((left.ndim - 1,), (1,)), ((), ())), preferred_element_type=jnp.float32
    )


def pool_exits(batch_rows, mask_of_valid, counts):
    total_value = jnp.einsum("ki,kiu->ku", mask_of_valid, batch_rows.astype(jnp.float32))
    return total_value / counts[:, None]


def spread_grad(exit_grad, mask_of_valid, counts):
    return mask_of_valid[:, :, None] * (exit_grad / counts[:, None])[:, None, :]


def matryoshka_losses(pooled, positives):
    pair_total = pooled.shape[0]
    target = (jnp.arange(pair_total, dtype=jnp.int32)[None, :] == positives[:, None]).astype(
        jnp.float32
    )
    losses = []
    for level_index in range(WIDTHS):
        leading_width = pooled.shape[-1] // 2**level_index
        query_vectors = pooled[:, 0, :leading_width]
        passage_rows = pooled[:, 1, :leading_width]
        query_vectors = query_vectors * lax.rsqrt(
            jnp.mean(query_vectors * query_vectors, axis=-1, keepdims=True) + 1e-06
        )
        passage_rows = passage_rows * lax.rsqrt(
            jnp.mean(passage_rows * passage_rows, axis=-1, keepdims=True) + 1e-06
        )
        score_matrix = jnp.dot(query_vectors, passage_rows.T, precision=lax.Precision.HIGHEST) / (
            leading_width * SOFTMAX_TEMPER
        )
        picked = jnp.sum(score_matrix * target, axis=-1)
        losses.append(jnp.mean(jax.nn.logsumexp(score_matrix, axis=-1) - picked))
    return jnp.stack(losses)


def pass_along(batch_rows, direction):
    return passed_along(batch_rows, "section", direction)


def forward_section(hidden, gain_vector, query_weight, key_weight, value_weight, out_weight):
    hidden_f = hidden.astype(jnp.float32)
    normed = normalize(hidden_f, gain_vector).astype(jnp.bfloat16)
    mixture = attend(
        jnp.dot(normed, query_weight, preferred_element_type=jnp.float32),
        jnp.dot(normed, key_weight, preferred_element_type=jnp.float32),
        jnp.dot(normed, value_weight, preferred_element_type=jnp.float32),
    ).astype(jnp.bfloat16)
    partial_value = jnp.dot(mixture, out_weight, preferred_element_type=jnp.float32)
    total_value = lax.psum(partial_value.astype(jnp.bfloat16), "mp").astype(jnp.float32)
    return (hidden_f + total_value).astype(jnp.bfloat16)


def backward_section(
    hidden, upstream, gain_vector, query_weight, key_weight, value_weight, out_weight
):
    hidden_f = hidden.astype(jnp.float32)
    inv_rms = lax.rsqrt(jnp.mean(hidden_f * hidden_f, axis=-1, keepdims=True) + EPSILON)
    normed = normalize(hidden_f, gain_vector).astype(jnp.bfloat16)
    out_grad = upstream.astype(jnp.bfloat16)
    mixture_f, pullback = jax.vjp(
        attend,
        jnp.dot(normed, query_weight, preferred_element_type=jnp.float32),
        jnp.dot(normed, key_weight, preferred_element_type=jnp.float32),
        jnp.dot(normed, value_weight, preferred_element_type=jnp.float32),
    )
    mixture = mixture_f.astype(jnp.bfloat16)
    mixture_grad = contract_last(out_grad, out_weight).astype(jnp.bfloat16)
    pulled = pullback(lax.optimization_barrier(mixture_grad).astype(jnp.float32))
    query_grad, key_grad, value_grad = [piece_grad.astype(jnp.bfloat16) for piece_grad in pulled]
    member_grad = (
        contract_last(query_grad, query_weight)
        + contract_last(key_grad, key_weight)
        + contract_last(value_grad, value_weight)
    )
    normed_grad = lax.psum(member_grad.astype(jnp.bfloat16), "mp").astype(jnp.float32)
    rounded = lax.optimization_barrier(member_grad.astype(jnp.bfloat16)).astype(jnp.float32)
    gain_term = jnp.sum(rounded * hidden_f * inv_rms, axis=(0, 1))
    _, norm_pull = jax.vjp(lambda values: normalize(values, gain_vector), hidden_f)
    input_grad = (upstream + norm_pull(normed_grad)[0]).astype(jnp.bfloat16)
    width_all = hidden.shape[-1]
    head_grads = jnp.concatenate([query_grad, key_grad, value_grad], axis=-1)
    stored_now = (
        normed.reshape(-1, width_all),
        out_grad.reshape(-1, width_all),
        head_grads.reshape(-1, head_grads.shape[-1]),
        mixture.reshape(-1, mixture.shape[-1]),
        gain_term,
    )
    return (input_grad, stored_now)


def local(entrance, lengths, positives, norm_gains, query_proj, key_proj, value_proj, out_proj):
    section_count = lax.axis_size("section")
    section_index = lax.axis_index("section")
    pair_count = entrance.shape[0]
    seq_count = 2 * pair_count
    length = entrance.shape[2]
    width_all = entrance.shape[3]
    start_hidden = entrance.reshape(seq_count, length, width_all)
    mask_of_valid = (
        jnp.arange(length, dtype=jnp.int32)[None, :] < lengths.reshape(seq_count, 1)
    ).astype(jnp.float32)
    counts = jnp.sum(mask_of_valid, axis=1)
    gain_vector = norm_gains[0]
    query_weight = query_proj[0]
    key_weight = key_proj[0]
    value_weight = value_proj[0]
    out_weight = out_proj[0]
    current = start_hidden
    saved_input = start_hidden
    exit_rows = start_hidden
    for section_turn in range(section_count):
        produced = forward_section(
            current, gain_vector, query_weight, key_weight, value_weight, out_weight
        )
        chosen = section_index == section_turn
        saved_input = jnp.where(chosen, current, saved_input)
        exit_rows = jnp.where(chosen, produced, exit_rows)
        if section_turn + 1 < section_count:
            arrived = pass_along(produced, 1)
            current = jnp.where(section_index == 0, start_hidden, arrived)
    pooled = pool_exits(exit_rows, mask_of_valid, counts).reshape(pair_count, 2, width_all)
    gathered = lax.all_gather(pooled.astype(jnp.bfloat16), "dp", axis=0, tiled=True).astype(
        pooled.dtype
    )
    losses_now, pullback = jax.vjp(
        lambda embedded: matryoshka_losses(embedded, positives), gathered
    )
    pair_grads = pullback(jnp.ones((WIDTHS,), jnp.float32))[0]
    own_losses = losses_now[None]
    own_grad = lax.dynamic_slice_in_dim(
        pair_grads, lax.axis_index("dp") * pair_count, pair_count, 0
    )
    token_grad = spread_grad(own_grad.reshape(seq_count, width_all), mask_of_valid, counts)
    incoming = jnp.zeros(start_hidden.shape, jnp.bfloat16)
    stored = None
    for section_turn in range(section_count):
        owner_section = section_count - 1 - section_turn
        upstream = token_grad + incoming.astype(jnp.float32)
        input_grad, stored_now = backward_section(
            saved_input, upstream, gain_vector, query_weight, key_weight, value_weight, out_weight
        )
        chosen = section_index == owner_section
        if stored is None:
            stored = stored_now
        else:
            stored = jax.tree.map(
                lambda fresh, former: jnp.where(chosen, fresh, former), stored_now, stored
            )
        if section_turn + 1 < section_count:
            incoming = pass_along(input_grad, -1)
    normed_rows, out_rows, head_grads, mixture_rows, gain_term = stored
    gain_share = lax.psum_scatter(gain_term, ("dp", "mp"), scatter_dimension=0, tiled=True)
    normed_cols, out_cols = (
        lax.all_to_all(normed_rows, "dp", split_axis=1, concat_axis=0, tiled=True),
        lax.all_to_all(out_rows, "dp", split_axis=1, concat_axis=0, tiled=True),
    )
    head_piece = lax.all_gather(head_grads, "dp", axis=0, tiled=True)
    mixture_piece = lax.all_gather(mixture_rows, "dp", axis=0, tiled=True)
    weight_sums = jnp.concatenate(
        [contract_rows(normed_cols, head_piece), contract_rows(out_cols, mixture_piece)], axis=1
    )
    query_cols = query_weight.shape[1]
    kv_cols = key_weight.shape[1]
    query_grad_out = weight_sums[:, :query_cols][None]
    key_grad_out = weight_sums[:, query_cols : query_cols + kv_cols][None]
    value_grad_out = weight_sums[:, query_cols + kv_cols : query_cols + 2 * kv_cols][None]
    out_grad_out = weight_sums[:, query_cols + 2 * kv_cols :].T[None]
    return (
        own_losses,
        gain_share[None],
        query_grad_out,
        key_grad_out,
        value_grad_out,
        out_grad_out,
    )


def solution(mesh):
    in_specs = (
        P("dp", None, None, None),
        P("dp", None),
        P(),
        P("section", None),
        P("section", None, "mp"),
        P("section", None, "mp"),
        P("section", None, "mp"),
        P("section", "mp", None),
    )
    out_specs = (
        P("section", None),
        P("section", ("dp", "mp")),
        P("section", "dp", "mp"),
        P("section", "dp", "mp"),
        P("section", "dp", "mp"),
        P("section", "mp", "dp"),
    )
    return jax.shard_map(local, mesh=mesh, in_specs=in_specs, out_specs=out_specs, check_vma=False)
```

profile of v0, /device:TPU:0, one launch (start us, length us, event | category | flops | bytes accessed | tf_op | source)
XLA Modules:
  0.0 794.6 jit_solution(6625503369172345784)
XLA Ops:
  9.4 6.4 copy.140
  27.7 45.7 %all-reduce.39.cloned.1.call-done = bf16[2,96,4096]{2,1,0:T(8,128)(2,1)} async-done(((bf16[2,96,4096]{2,1,0:T(8,128)(2,1)}), bf16[2,96,4096]{2,1,0:T(8,128)(2,1)}) %all-reduce.39.cloned.1.call-update) | async-done | bytes 1572880 | tf_op jit(solution)/shard_map/psum | solution.py:129
  76.5 4.5 collective-permute-start
  81.0 32.7 %collective-permute-done = bf16[2,96,4096]{2,1,0:T(8,128)(2,1)} collective-permute-done((bf16[2,96,4096]{2,1,0:T(8,128)(2,1)}, bf16[2,96,4096]{2,1,0:T(8,128)(2,1)}, u32[]{:S(2)}, u32[]{:S(2)}) %collective-permute-start) | collective-permute-done | bytes 1572896 | tf_op jit(solution)/shard_map/ppermute | solution.py:16
  124.4 45.4 %all-reduce.41.cloned.1.call-done = bf16[2,96,4096]{2,1,0:T(8,128)(2,1)} async-done(((bf16[2,96,4096]{2,1,0:T(8,128)(2,1)}), bf16[2,96,4096]{2,1,0:T(8,128)(2,1)}) %all-reduce.41.cloned.1.call-update) | async-done | bytes 1572880 | tf_op jit(solution)/shard_map/psum | solution.py:129
  176.2 33.3 %collective-permute-done.1 = bf16[2,96,4096]{2,1,0:T(8,128)(2,1)S(1)} collective-permute-done((bf16[2,96,4096]{2,1,0:T(8,128)(2,1)S(1)}, bf16[2,96,4096]{2,1,0:T(8,128)(2,1)S(1)}, u32[]{:S(2)}, u32[]{:S(2)}) %collective-permute-start.1) | collective-permute-done | bytes 1572896 | tf_op jit(solution)/shard_map/ppermute | solution.py:16
  220.2 44.0 %all-reduce.43.cloned.1.call-done = bf16[2,96,4096]{2,1,0:T(8,128)(2,1)} async-done(((bf16[2,96,4096]{2,1,0:T(8,128)(2,1)}), bf16[2,96,4096]{2,1,0:T(8,128)(2,1)}) %all-reduce.43.cloned.1.call-update) | async-done | bytes 1572880 | tf_op jit(solution)/shard_map/psum | solution.py:129
  273.3 31.3 %collective-permute-done.2 = bf16[2,96,4096]{2,1,0:T(8,128)(2,1)} collective-permute-done((bf16[2,96,4096]{2,1,0:T(8,128)(2,1)}, bf16[2,96,4096]{2,1,0:T(8,128)(2,1)}, u32[]{:S(2)}, u32[]{:S(2)}) %collective-permute-start.2) | collective-permute-done | bytes 1572896 | tf_op jit(solution)/shard_map/ppermute | solution.py:16
  326.7 41.8 %all-reduce.45.cloned.1.call-done = bf16[2,96,4096]{2,1,0:T(8,128)(2,1)} async-done(((bf16[2,96,4096]{2,1,0:T(8,128)(2,1)}), bf16[2,96,4096]{2,1,0:T(8,128)(2,1)}) %all-reduce.45.cloned.1.call-update) | async-done | bytes 1572880 | tf_op jit(solution)/shard_map/psum | solution.py:129
  373.0 4.6 all-gather.1
  402.4 43.0 %all-reduce.47.cloned.1.call-done = bf16[2,96,4096]{2,1,0:T(8,128)(2,1)} async-done(((bf16[2,96,4096]{2,1,0:T(8,128)(2,1)}), bf16[2,96,4096]{2,1,0:T(8,128)(2,1)}) %all-reduce.47.cloned.1.call-update) | async-done | bytes 1572880 | tf_op jit(solution)/shard_map/psum | solution.py:155
  451.2 36.2 %collective-permute-done.3 = bf16[2,96,4096]{2,1,0:T(8,128)(2,1)S(1)} collective-permute-done((bf16[2,96,4096]{2,1,0:T(8,128)(2,1)S(1)}, bf16[2,96,4096]{2,1,0:T(8,128)(2,1)S(1)}, u32[]{:S(2)}, u32[]{:S(2)}) %collective-permute-start.3) | collective-permute-done | bytes 1572896 | tf_op jit(solution)/shard_map/ppermute | solution.py:16
  503.0 42.1 %all-reduce.49.cloned.1.call-done = bf16[2,96,4096]{2,1,0:T(8,128)(2,1)} async-done(((bf16[2,96,4096]{2,1,0:T(8,128)(2,1)}), bf16[2,96,4096]{2,1,0:T(8,128)(2,1)}) %all-reduce.49.cloned.1.call-update) | async-done | bytes 1572880 | tf_op jit(solution)/shard_map/psum | solution.py:155
  550.4 36.4 %collective-permute-done.4 = bf16[2,96,4096]{2,1,0:T(8,128)(2,1)S(1)} collective-permute-done((bf16[2,96,4096]{2,1,0:T(8,128)(2,1)S(1)}, bf16[2,96,4096]{2,1,0:T(8,128)(2,1)S(1)}, u32[]{:S(2)}, u32[]{:S(2)}) %collective-permute-start.4) | collective-permute-done | bytes 1572896 | tf_op jit(solution)/shard_map/ppermute | solution.py:16
  602.5 42.2 %all-reduce.51.cloned.1.call-done = bf16[2,96,4096]{2,1,0:T(8,128)(2,1)} async-done(((bf16[2,96,4096]{2,1,0:T(8,128)(2,1)}), bf16[2,96,4096]{2,1,0:T(8,128)(2,1)}) %all-reduce.51.cloned.1.call-update) | async-done | bytes 1572880 | tf_op jit(solution)/shard_map/psum | solution.py:155
  661.1 4.6 all-to-all-start
  676.2 5.6 mul.2560
  682.4 9.3 %all_gather.11 = bf16[384,512]{1,0:T(8,128)(2,1)} all-gather(bf16[192,512]{1,0:T(8,128)(2,1)} %bitcast.1023), channel_id=1, replica_groups=mesh['section'=4,'dp'=2,'mp'=4] {'dp'}, dimensions={0}, use_global_device_ids=true | all-gather | bytes 589824 | tf_op jit(solution)/shard_map/all_gather | solution.py:239
  723.2 8.6 %all_gather.10 = bf16[384,768]{1,0:T(8,128)(2,1)S(1)} all-gather(bf16[192,768]{1,0:T(8,128)(2,1)S(1)} %maximum_select_fusion), channel_id=1, replica_groups=mesh['section'=4,'dp'=2,'mp'=4] {'dp'}, dimensions={0}, use_global_device_ids=true | all-gather | bytes 884736 | tf_op jit(solution)/shard_map/all_gather | solution.py:238
  731.8 5.4 fusion.63
  737.1 4.9 all-to-all-start.1
  752.7 24.6 %all-reduce.30 = f32[4096]{0:T(1024)S(1)} all-reduce(f32[4096]{0:T(1024)S(1)} %select_select_fusion), channel_id=3, replica_groups=mesh['section'=4,'dp'=2,'mp'=4] {'dp','mp'}, use_global_device_ids=true, to_apply=%region_90.91.clone | all-reduce | flops 4096 | bytes 32768
  777.9 4.7 slice_bitcast_fusion
  782.6 4.7 convolution_bitcast_fusion
  (496 shorter events, 210.8 us)
Async XLA Ops:
  7.2 66.2 %all-reduce.39.cloned.1.call-start = ((), (), s32[]{:S(2)}) async-start(), calls=%async_computation.2 | async-start | bytes 3145728 | tf_op jit(solution)/shard_map/psum | solution.py:129
  7.3 317.0 %copy-start.62 = (pred[96,96]{0,1:T(8,128)(4,1)}, pred[96,96]{0,1:T(8,128)(4,1)S(1)}, u32[]{:S(2)}) copy-start(pred[96,96]{0,1:T(8,128)(4,1)S(1)} %iota_compare_fusion) | copy-start | bytes 27652
  27.6 142.1 %all-reduce.41.cloned.1.call-start = ((), (), s32[]{:S(2)}) async-start(), calls=%async_computation.3 | async-start | bytes 3145728 | tf_op jit(solution)/shard_map/psum | solution.py:129
  76.5 37.2 %collective-permute-start = (bf16[2,96,4096]{2,1,0:T(8,128)(2,1)}, bf16[2,96,4096]{2,1,0:T(8,128)(2,1)}, u32[]{:S(2)}, u32[]{:S(2)}) collective-permute-start(bf16[2,96,4096]{2,1,0:T(8,128)(2,1)} %fusion.25), channel_id=1, source_target_pairs={{0,8},{8,16},{16,24},{1,9},{9,17},{17,25},{2,10},{10,18},{18,26},{... | collective-permute-start | bytes 4718600 | tf_op jit(solution)/shard_map/ppermute | solution.py:16
  124.3 140.0 %all-reduce.43.cloned.1.call-start = ((), (), s32[]{:S(2)}) async-start(), calls=%async_computation.4 | async-start | bytes 3145728 | tf_op jit(solution)/shard_map/psum | solution.py:129
  172.2 37.2 %collective-permute-start.1 = (bf16[2,96,4096]{2,1,0:T(8,128)(2,1)S(1)}, bf16[2,96,4096]{2,1,0:T(8,128)(2,1)S(1)}, u32[]{:S(2)}, u32[]{:S(2)}) collective-permute-start(bf16[2,96,4096]{2,1,0:T(8,128)(2,1)S(1)} %fusion.29), channel_id=1, source_target_pairs={{0,8},{8,16},{16,24},{1,9},{9,17},{17,25},{2,10},{10,18},{18,26},{... | collective-permute-start | bytes 4718600 | tf_op jit(solution)/shard_map/ppermute | solution.py:16
  215.7 48.6 %copy-start.24 = (bf16[2,96,4096]{2,1,0:T(8,128)(2,1)S(1)}, bf16[2,96,4096]{2,1,0:T(8,128)(2,1)}, u32[]{:S(2)}) copy-start(bf16[2,96,4096]{2,1,0:T(8,128)(2,1)} %copy-done.23) | copy-start | bytes 4718596
  220.2 51.8 %copy-start.114 = (s32[1,2]{1,0:T(1,128)S(1)}, s32[1,2]{1,0:T(1,128)}, u32[]{:S(2)}) copy-start(s32[1,2]{1,0:T(1,128)} %param.9) | copy-start | bytes 28
  220.2 148.3 %all-reduce.45.cloned.1.call-start = ((), (), s32[]{:S(2)}) async-start(), calls=%async_computation.5 | async-start | bytes 3145728 | tf_op jit(solution)/shard_map/psum | solution.py:129
  267.4 37.2 %collective-permute-start.2 = (bf16[2,96,4096]{2,1,0:T(8,128)(2,1)}, bf16[2,96,4096]{2,1,0:T(8,128)(2,1)}, u32[]{:S(2)}, u32[]{:S(2)}) collective-permute-start(bf16[2,96,4096]{2,1,0:T(8,128)(2,1)} %fusion.33), channel_id=1, source_target_pairs={{0,8},{8,16},{16,24},{1,9},{9,17},{17,25},{2,10},{10,18},{18,26},{... | collective-permute-start | bytes 4718600 | tf_op jit(solution)/shard_map/ppermute | solution.py:16
  323.9 121.5 %all-reduce.47.cloned.1.call-start = ((), (), s32[]{:S(2)}) async-start(), calls=%async_computation.6 | async-start | bytes 3145728 | tf_op jit(solution)/shard_map/psum | solution.py:155
  324.3 71.7 %copy-start.60 = (bf16[2,96,4,128]{3,1,2,0:T(8,128)(2,1)}, bf16[2,96,4,128]{3,1,2,0:T(8,128)(2,1)S(1)}, u32[]{:S(2)}) copy-start(bf16[2,96,4,128]{3,1,2,0:T(8,128)(2,1)S(1)} %pad_maximum_fusion) | copy-start | bytes 589828
  324.6 71.7 %copy-start.88 = (f32[2,4,96]{2,1,0:T(4,128)}, f32[2,4,96]{2,1,0:T(4,128)S(1)}, u32[]{:S(2)}) copy-start(f32[2,4,96]{2,1,0:T(4,128)S(1)} %get-tuple-element.178) | copy-start | bytes 9220
  324.7 71.6 %copy-start.103 = (f32[2,4,96]{2,1,0:T(4,128)}, f32[2,4,96]{2,1,0:T(4,128)S(1)}, u32[]{:S(2)}) copy-start(f32[2,4,96]{2,1,0:T(4,128)S(1)} %fusion.513) | copy-start | bytes 9220
  324.7 69.9 %copy-start.92 = (f32[2,4,96]{2,1,0:T(4,128)}, f32[2,4,96]{2,1,0:T(4,128)S(1)}, u32[]{:S(2)}) copy-start(f32[2,4,96]{2,1,0:T(4,128)S(1)} %multiply_divide_fusion) | copy-start | bytes 9220
  326.7 68.0 %copy-start.53 = (bf16[2,96,128,1]{2,1,3,0:T(8,128)(2,1)}, bf16[2,96,128,1]{2,1,3,0:T(8,128)(2,1)S(1)}, u32[]{:S(2)}) copy-start(bf16[2,96,128,1]{2,1,3,0:T(8,128)(2,1)S(1)} %fusion.144) | copy-start | bytes 147460
  402.4 142.8 %all-reduce.49.cloned.1.call-start = ((), (), s32[]{:S(2)}) async-start(), calls=%async_computation.7 | async-start | bytes 3145728 | tf_op jit(solution)/shard_map/psum | solution.py:155
  449.4 38.0 %collective-permute-start.3 = (bf16[2,96,4096]{2,1,0:T(8,128)(2,1)S(1)}, bf16[2,96,4096]{2,1,0:T(8,128)(2,1)S(1)}, u32[]{:S(2)}, u32[]{:S(2)}) collective-permute-start(bf16[2,96,4096]{2,1,0:T(8,128)(2,1)S(1)} %fusion.42), channel_id=1, source_target_pairs={{8,0},{16,8},{24,16},{9,1},{17,9},{25,17},{10,2},{18,10},{26,18},{... | collective-permute-start | bytes 4718600 | tf_op jit(solution)/shard_map/ppermute | solution.py:16
  503.0 141.7 %all-reduce.51.cloned.1.call-start = ((), (), s32[]{:S(2)}) async-start(), calls=%async_computation.8 | async-start | bytes 3145728 | tf_op jit(solution)/shard_map/psum | solution.py:155
  547.5 42.2 %copy-start.7 = (bf16[1,512,4096]{2,1,0:T(8,128)(2,1)S(1)}, bf16[1,512,4096]{2,1,0:T(8,128)(2,1)}, u32[]{:S(2)}) copy-start(bf16[1,512,4096]{2,1,0:T(8,128)(2,1)} %param.15) | copy-start | bytes 12582916
  548.9 37.9 %collective-permute-start.4 = (bf16[2,96,4096]{2,1,0:T(8,128)(2,1)S(1)}, bf16[2,96,4096]{2,1,0:T(8,128)(2,1)S(1)}, u32[]{:S(2)}, u32[]{:S(2)}) collective-permute-start(bf16[2,96,4096]{2,1,0:T(8,128)(2,1)S(1)} %fusion.39), channel_id=1, source_target_pairs={{8,0},{16,8},{24,16},{9,1},{17,9},{25,17},{10,2},{18,10},{26,18},{... | collective-permute-start | bytes 4718600 | tf_op jit(solution)/shard_map/ppermute | solution.py:16
  649.6 53.3 %collective-permute-start.5 = (bf16[2,96,4096]{2,1,0:T(8,128)(2,1)}, bf16[2,96,4096]{2,1,0:T(8,128)(2,1)}, u32[]{:S(2)}, u32[]{:S(2)}) collective-permute-start(bf16[2,96,4096]{2,1,0:T(8,128)(2,1)} %fusion.41), channel_id=1, source_target_pairs={{8,0},{16,8},{24,16},{9,1},{17,9},{25,17},{10,2},{18,10},{26,18},{... | collective-permute-start | bytes 4718600 | tf_op jit(solution)/shard_map/ppermute | solution.py:16
  661.1 76.0 %all-to-all-start = ((bf16[192,2,2048]{2,0,1:T(8,128)(2,1)}), bf16[192,2,2048]{2,0,1:T(8,128)(2,1)}, u32[]{:S(2)}, u32[]{:S(2)}) async-start(bf16[192,2,2048]{2,0,1:T(8,128)(2,1)} %copy.95), calls=%async_computation | async-start | bytes 3145728 | tf_op jit(solution)/shard_map/all_to_all | solution.py:235
  737.1 45.5 %all-to-all-start.1 = ((bf16[192,2,2048]{2,0,1:T(8,128)(2,1)}), bf16[192,2,2048]{2,0,1:T(8,128)(2,1)}, u32[]{:S(2)}, u32[]{:S(2)}) async-start(bf16[192,2,2048]{2,0,1:T(8,128)(2,1)} %fusion.63), calls=%async_computation.1 | async-start | bytes 3145728 | tf_op jit(solution)/shard_map/all_to_all | solution.py:236
  (106 other events, 641.8 us)
Sparse Core Ops, SparseCore 0:
  27.8 45.5 all-reduce.38
  124.4 45.3 all-reduce.40
  220.3 43.9 all-reduce.42
  324.1 44.3 all-reduce.44
  402.5 42.9 all-reduce.46
  503.1 41.9 all-reduce.48
  602.6 41.9 all-reduce.50
where the time goes:
time: 805 us; the launch traced here: 795 us
  waiting for transfers between devices  474 us (59%)
  matrix products  102 us (13%)
  local copies, waits for them, and re-layouts  66.7 us (8%)
  other arithmetic  55.3 us (7%)
  blocking collectives  47.1 us (6%)
  starting transfers between devices  27.3 us (3%)
  between operations  21.9 us (3%)
    psum x4, waiting for transfers between devices, forward_section(): lax.psum(partial_value.astype(jnp.bfloat16), 'mp').astype(jnp.float32)  177 us
    ppermute x6, waiting for transfers between devices, passed_along(): lax.ppermute(value, axis, [(source, source + steps) for source in range(f...  170 us
    psum x3, waiting for transfers between devices, backward_section(): lax.psum(member_grad.astype(jnp.bfloat16), 'mp').astype(jnp.float32)  127 us
    unnamed x1, blocking collectives  24.6 us
    dot_general x16, matrix products, contract_last(): lax.dot_general(left, right, (((left.ndim - 1,), (1,)), ((), ())), prefer...  24.5 us
    unnamed x237, local copies, waits for them, and re-layouts  18.1 us
    dot_general x13, matrix products, attend(): jnp.einsum('skgij,sjke->sikge', weights.astype(jnp.float32), values.astyp...  17.9 us
    ppermute x6, starting transfers between devices, passed_along(): lax.ppermute(value, axis, [(source, source + steps) for source in range(f...  17.6 us
  transfers between devices with their start and end apart: 15, of which 12 were waited for; matrix products, arithmetic and copies ran while one was open for 9% of the time, Pallas kernels for 0%

commit v1 on v0

--- a/solution.py
+++ b/solution.py
@@ -8,6 +8,12 @@
 EPSILON = 1e-05
 SOFTMAX_TEMPER = 0.05
 ROPE_BASE = 500000.0
+
+
+def summed_here(block, axis):
+    parts = lax.all_gather(block, axis, axis=0, tiled=False)
+    result = parts.sum(axis=0)
+    return result
 
 
 def passed_along(value, axis, steps):
@@ -152,7 +158,7 @@
         + contract_last(key_grad, key_weight)
         + contract_last(value_grad, value_weight)
     )
-    normed_grad = lax.psum(member_grad.astype(jnp.bfloat16), "mp").astype(jnp.float32)
+    normed_grad = summed_here(member_grad.astype(jnp.bfloat16), "mp").astype(jnp.float32)
     rounded = lax.optimization_barrier(member_grad.astype(jnp.bfloat16)).astype(jnp.float32)
     gain_term = jnp.sum(rounded * hidden_f * inv_rms, axis=(0, 1))
     _, norm_pull = jax.vjp(lambda values: normalize(values, gain_vector), hidden_f)

time: 805 us -> 835 us (1.037)
  other arithmetic: 55.3 us -> 72 us
  waiting for transfers between devices: 474 us -> 486 us
    all_gather x0 -> x3, waiting for transfers between devices: none -> 138 us  [summed_here(): parts = lax.all_gather(block, axis, axis=0, tiled=False)]
    psum x3 -> x0, waiting for transfers between devices: 127 us -> none  [backward_section(): lax.psum(member_grad.astype(jnp.bfloat16), 'mp').astype(jnp.float32)]
    reduce_sum x0 -> x3, other arithmetic: none -> 16.7 us  [summed_here(): result = parts.sum(axis=0)]
  transfers between devices with their start and end apart: 15 -> 15, of which waited for: 12 -> 12; matrix products, arithmetic and copies ran while one was open for 9% -> 8% of each run, Pallas kernels for 0% -> 0%
where the time goes in v1:
time: 835 us; the launch traced here: 824 us
  waiting for transfers between devices  486 us (58%)
  matrix products  102 us (12%)
  other arithmetic  72 us (9%)
  local copies, waits for them, and re-layouts  66.7 us (8%)
  blocking collectives  49.1 us (6%)
  starting transfers between devices  27.1 us (3%)
  between operations  21.6 us (3%)
    psum x4, waiting for transfers between devices, forward_section(): lax.psum(partial_value.astype(jnp.bfloat16), 'mp').astype(jnp.float32)  177 us
    ppermute x6, waiting for transfers between devices, passed_along(): lax.ppermute(value, axis, [(source, source + steps) for source in range(f...  171 us
    all_gather x3, waiting for transfers between devices, summed_here(): parts = lax.all_gather(block, axis, axis=0, tiled=False)  138 us
    unnamed x1, blocking collectives  25.1 us
    dot_general x16, matrix products, contract_last(): lax.dot_general(left, right, (((left.ndim - 1,), (1,)), ((), ())), prefer...  24.5 us
    unnamed x237, local copies, waits for them, and re-layouts  18.1 us
    dot_general x13, matrix products, attend(): jnp.einsum('skgij,sjke->sikge', weights.astype(jnp.float32), values.astyp...  17.9 us
    dot_general x4, matrix products, forward_section(): jnp.dot(mixture, out_weight, preferred_element_type=jnp.float32)  17.5 us
  transfers between devices with their start and end apart: 15, of which 12 were waited for; matrix products, arithmetic and copies ran while one was open for 8% of the time, Pallas kernels for 0%

profile of v1, /device:TPU:0, one launch (start us, length us, event | category | flops | bytes accessed | tf_op | source)
XLA Modules:
  0.0 824.3 jit_solution(13228710092608984793)
XLA Ops:
  9.4 6.4 copy.140
  27.7 45.7 %all-reduce.36.cloned.1.call-done = bf16[2,96,4096]{2,1,0:T(8,128)(2,1)} async-done(((bf16[2,96,4096]{2,1,0:T(8,128)(2,1)}), bf16[2,96,4096]{2,1,0:T(8,128)(2,1)}) %all-reduce.36.cloned.1.call-update) | async-done | bytes 1572880 | tf_op jit(solution)/shard_map/psum | solution.py:135
  81.0 32.7 %collective-permute-done = bf16[2,96,4096]{2,1,0:T(8,128)(2,1)} collective-permute-done((bf16[2,96,4096]{2,1,0:T(8,128)(2,1)}, bf16[2,96,4096]{2,1,0:T(8,128)(2,1)}, u32[]{:S(2)}, u32[]{:S(2)}) %collective-permute-start) | collective-permute-done | bytes 1572896 | tf_op jit(solution)/shard_map/ppermute | solution.py:22
  124.4 45.4 %all-reduce.38.cloned.1.call-done = bf16[2,96,4096]{2,1,0:T(8,128)(2,1)} async-done(((bf16[2,96,4096]{2,1,0:T(8,128)(2,1)}), bf16[2,96,4096]{2,1,0:T(8,128)(2,1)}) %all-reduce.38.cloned.1.call-update) | async-done | bytes 1572880 | tf_op jit(solution)/shard_map/psum | solution.py:135
  176.2 33.2 %collective-permute-done.1 = bf16[2,96,4096]{2,1,0:T(8,128)(2,1)S(1)} collective-permute-done((bf16[2,96,4096]{2,1,0:T(8,128)(2,1)S(1)}, bf16[2,96,4096]{2,1,0:T(8,128)(2,1)S(1)}, u32[]{:S(2)}, u32[]{:S(2)}) %collective-permute-start.1) | collective-permute-done | bytes 1572896 | tf_op jit(solution)/shard_map/ppermute | solution.py:22
  220.2 44.0 %all-reduce.40.cloned.1.call-done = bf16[2,96,4096]{2,1,0:T(8,128)(2,1)} async-done(((bf16[2,96,4096]{2,1,0:T(8,128)(2,1)}), bf16[2,96,4096]{2,1,0:T(8,128)(2,1)}) %all-reduce.40.cloned.1.call-update) | async-done | bytes 1572880 | tf_op jit(solution)/shard_map/psum | solution.py:135
  273.2 31.3 %collective-permute-done.2 = bf16[2,96,4096]{2,1,0:T(8,128)(2,1)} collective-permute-done((bf16[2,96,4096]{2,1,0:T(8,128)(2,1)}, bf16[2,96,4096]{2,1,0:T(8,128)(2,1)}, u32[]{:S(2)}, u32[]{:S(2)}) %collective-permute-start.2) | collective-permute-done | bytes 1572896 | tf_op jit(solution)/shard_map/ppermute | solution.py:22
  326.6 41.8 %all-reduce.42.cloned.1.call-done = bf16[2,96,4096]{2,1,0:T(8,128)(2,1)} async-done(((bf16[2,96,4096]{2,1,0:T(8,128)(2,1)}), bf16[2,96,4096]{2,1,0:T(8,128)(2,1)}) %all-reduce.42.cloned.1.call-update) | async-done | bytes 1572880 | tf_op jit(solution)/shard_map/psum | solution.py:135
  372.9 4.8 all-gather.4
  402.5 46.5 %all-gather.9.cloned.1.call-done = bf16[8,96,4096]{2,1,0:T(8,128)(2,1)} async-done(((bf16[2,96,4096]{2,1,0:T(8,128)(2,1)}), bf16[8,96,4096]{2,1,0:T(8,128)(2,1)}) %all-gather.9.cloned.1.call-update) | async-done | bytes 6291472 | tf_op jit(solution)/shard_map/all_gather | solution.py:14
  449.0 5.6 reduce_sum.872
  460.1 37.0 %collective-permute-done.3 = bf16[2,96,4096]{2,1,0:T(8,128)(2,1)S(1)} collective-permute-done((bf16[2,96,4096]{2,1,0:T(8,128)(2,1)S(1)}, bf16[2,96,4096]{2,1,0:T(8,128)(2,1)S(1)}, u32[]{:S(2)}, u32[]{:S(2)}) %collective-permute-start.3) | collective-permute-done | bytes 1572896 | tf_op jit(solution)/shard_map/ppermute | solution.py:22
  512.8 45.5 %all-gather.11.cloned.1.call-done = bf16[8,96,4096]{2,1,0:T(8,128)(2,1)} async-done(((bf16[2,96,4096]{2,1,0:T(8,128)(2,1)}), bf16[8,96,4096]{2,1,0:T(8,128)(2,1)}) %all-gather.11.cloned.1.call-update) | async-done | bytes 6291472 | tf_op jit(solution)/shard_map/all_gather | solution.py:14
  558.4 5.6 reduce_sum.875
  569.2 36.9 %collective-permute-done.4 = bf16[2,96,4096]{2,1,0:T(8,128)(2,1)S(1)} collective-permute-done((bf16[2,96,4096]{2,1,0:T(8,128)(2,1)S(1)}, bf16[2,96,4096]{2,1,0:T(8,128)(2,1)S(1)}, u32[]{:S(2)}, u32[]{:S(2)}) %collective-permute-start.4) | collective-permute-done | bytes 1572896 | tf_op jit(solution)/shard_map/ppermute | solution.py:22
  621.8 45.6 %all-gather.13.cloned.1.call-done = bf16[8,96,4096]{2,1,0:T(8,128)(2,1)} async-done(((bf16[2,96,4096]{2,1,0:T(8,128)(2,1)}), bf16[8,96,4096]{2,1,0:T(8,128)(2,1)}) %all-gather.13.cloned.1.call-update) | async-done | bytes 6291472 | tf_op jit(solution)/shard_map/all_gather | solution.py:14
  667.4 5.6 reduce_sum.878
  704.5 5.6 mul.2560
  710.7 10.0 %all_gather.35 = bf16[384,512]{1,0:T(8,128)(2,1)} all-gather(bf16[192,512]{1,0:T(8,128)(2,1)} %bitcast.1029), channel_id=1, replica_groups=mesh['section'=4,'dp'=2,'mp'=4] {'dp'}, dimensions={0}, use_global_device_ids=true | all-gather | bytes 589824 | tf_op jit(solution)/shard_map/all_gather | solution.py:245
  752.2 9.1 %all_gather.34 = bf16[384,768]{1,0:T(8,128)(2,1)S(1)} all-gather(bf16[192,768]{1,0:T(8,128)(2,1)S(1)} %maximum_select_fusion), channel_id=1, replica_groups=mesh['section'=4,'dp'=2,'mp'=4] {'dp'}, dimensions={0}, use_global_device_ids=true | all-gather | bytes 884736 | tf_op jit(solution)/shard_map/all_gather | solution.py:244
  761.3 5.4 fusion.63
  766.7 4.8 all-to-all-start.1
  782.1 25.1 %all-reduce.30 = f32[4096]{0:T(1024)S(1)} all-reduce(f32[4096]{0:T(1024)S(1)} %select_select_fusion), channel_id=6, replica_groups=mesh['section'=4,'dp'=2,'mp'=4] {'dp','mp'}, use_global_device_ids=true, to_apply=%region_90.91.clone | all-reduce | flops 4096 | bytes 32768
  812.6 4.7 convolution_bitcast_fusion
  (499 shorter events, 224.4 us)
Async XLA Ops:
  7.2 66.2 %all-reduce.36.cloned.1.call-start = ((), (), s32[]{:S(2)}) async-start(), calls=%async_computation.2 | async-start | bytes 3145728 | tf_op jit(solution)/shard_map/psum | solution.py:135
  7.3 316.9 %copy-start.62 = (pred[96,96]{0,1:T(8,128)(4,1)}, pred[96,96]{0,1:T(8,128)(4,1)S(1)}, u32[]{:S(2)}) copy-start(pred[96,96]{0,1:T(8,128)(4,1)S(1)} %iota_compare_fusion) | copy-start | bytes 27652
  27.6 142.1 %all-reduce.38.cloned.1.call-start = ((), (), s32[]{:S(2)}) async-start(), calls=%async_computation.3 | async-start | bytes 3145728 | tf_op jit(solution)/shard_map/psum | solution.py:135
  76.5 37.2 %collective-permute-start = (bf16[2,96,4096]{2,1,0:T(8,128)(2,1)}, bf16[2,96,4096]{2,1,0:T(8,128)(2,1)}, u32[]{:S(2)}, u32[]{:S(2)}) collective-permute-start(bf16[2,96,4096]{2,1,0:T(8,128)(2,1)} %fusion.25), channel_id=1, source_target_pairs={{0,8},{8,16},{16,24},{1,9},{9,17},{17,25},{2,10},{10,18},{18,26},{... | collective-permute-start | bytes 4718600 | tf_op jit(solution)/shard_map/ppermute | solution.py:22
  124.3 139.9 %all-reduce.40.cloned.1.call-start = ((), (), s32[]{:S(2)}) async-start(), calls=%async_computation.4 | async-start | bytes 3145728 | tf_op jit(solution)/shard_map/psum | solution.py:135
  172.2 37.2 %collective-permute-start.1 = (bf16[2,96,4096]{2,1,0:T(8,128)(2,1)S(1)}, bf16[2,96,4096]{2,1,0:T(8,128)(2,1)S(1)}, u32[]{:S(2)}, u32[]{:S(2)}) collective-permute-start(bf16[2,96,4096]{2,1,0:T(8,128)(2,1)S(1)} %fusion.29), channel_id=1, source_target_pairs={{0,8},{8,16},{16,24},{1,9},{9,17},{17,25},{2,10},{10,18},{18,26},{... | collective-permute-start | bytes 4718600 | tf_op jit(solution)/shard_map/ppermute | solution.py:22
  215.7 48.5 %copy-start.27 = (bf16[2,96,4096]{2,1,0:T(8,128)(2,1)S(1)}, bf16[2,96,4096]{2,1,0:T(8,128)(2,1)}, u32[]{:S(2)}) copy-start(bf16[2,96,4096]{2,1,0:T(8,128)(2,1)} %copy-done.26) | copy-start | bytes 4718596
  220.1 51.7 %copy-start.114 = (s32[1,2]{1,0:T(1,128)S(1)}, s32[1,2]{1,0:T(1,128)}, u32[]{:S(2)}) copy-start(s32[1,2]{1,0:T(1,128)} %param.9) | copy-start | bytes 28
  220.1 148.3 %all-reduce.42.cloned.1.call-start = ((), (), s32[]{:S(2)}) async-start(), calls=%async_computation.5 | async-start | bytes 3145728 | tf_op jit(solution)/shard_map/psum | solution.py:135
  267.3 37.2 %collective-permute-start.2 = (bf16[2,96,4096]{2,1,0:T(8,128)(2,1)}, bf16[2,96,4096]{2,1,0:T(8,128)(2,1)}, u32[]{:S(2)}, u32[]{:S(2)}) collective-permute-start(bf16[2,96,4096]{2,1,0:T(8,128)(2,1)} %fusion.33), channel_id=1, source_target_pairs={{0,8},{8,16},{16,24},{1,9},{9,17},{17,25},{2,10},{10,18},{18,26},{... | collective-permute-start | bytes 4718600 | tf_op jit(solution)/shard_map/ppermute | solution.py:22
  323.9 125.2 %all-gather.9.cloned.1.call-start = ((), (), s32[]{:S(2)}) async-start(), calls=%async_computation.6 | async-start | bytes 7864320 | tf_op jit(solution)/shard_map/all_gather | solution.py:14
  324.2 71.9 %copy-start.60 = (bf16[2,96,4,128]{3,1,2,0:T(8,128)(2,1)}, bf16[2,96,4,128]{3,1,2,0:T(8,128)(2,1)S(1)}, u32[]{:S(2)}) copy-start(bf16[2,96,4,128]{3,1,2,0:T(8,128)(2,1)S(1)} %pad_maximum_fusion) | copy-start | bytes 589828
  324.5 71.9 %copy-start.88 = (f32[2,4,96]{2,1,0:T(4,128)}, f32[2,4,96]{2,1,0:T(4,128)S(1)}, u32[]{:S(2)}) copy-start(f32[2,4,96]{2,1,0:T(4,128)S(1)} %get-tuple-element.178) | copy-start | bytes 9220
  324.7 71.8 %copy-start.103 = (f32[2,4,96]{2,1,0:T(4,128)}, f32[2,4,96]{2,1,0:T(4,128)S(1)}, u32[]{:S(2)}) copy-start(f32[2,4,96]{2,1,0:T(4,128)S(1)} %fusion.513) | copy-start | bytes 9220
  324.7 70.1 %copy-start.92 = (f32[2,4,96]{2,1,0:T(4,128)}, f32[2,4,96]{2,1,0:T(4,128)S(1)}, u32[]{:S(2)}) copy-start(f32[2,4,96]{2,1,0:T(4,128)S(1)} %multiply_divide_fusion) | copy-start | bytes 9220
  326.6 68.1 %copy-start.53 = (bf16[2,96,128,1]{2,1,3,0:T(8,128)(2,1)}, bf16[2,96,128,1]{2,1,3,0:T(8,128)(2,1)S(1)}, u32[]{:S(2)}) copy-start(bf16[2,96,128,1]{2,1,3,0:T(8,128)(2,1)S(1)} %fusion.144) | copy-start | bytes 147460
  402.5 155.9 %all-gather.11.cloned.1.call-start = ((), (), s32[]{:S(2)}) async-start(), calls=%async_computation.7 | async-start | bytes 7864320 | tf_op jit(solution)/shard_map/all_gather | solution.py:14
  458.5 38.6 %collective-permute-start.3 = (bf16[2,96,4096]{2,1,0:T(8,128)(2,1)S(1)}, bf16[2,96,4096]{2,1,0:T(8,128)(2,1)S(1)}, u32[]{:S(2)}, u32[]{:S(2)}) collective-permute-start(bf16[2,96,4096]{2,1,0:T(8,128)(2,1)S(1)} %fusion.42), channel_id=1, source_target_pairs={{8,0},{16,8},{24,16},{9,1},{17,9},{25,17},{10,2},{18,10},{26,18},{... | collective-permute-start | bytes 4718600 | tf_op jit(solution)/shard_map/ppermute | solution.py:22
  512.8 154.6 %all-gather.13.cloned.1.call-start = ((), (), s32[]{:S(2)}) async-start(), calls=%async_computation.8 | async-start | bytes 7864320 | tf_op jit(solution)/shard_map/all_gather | solution.py:14
  566.3 42.7 %copy-start.7 = (bf16[1,512,4096]{2,1,0:T(8,128)(2,1)S(1)}, bf16[1,512,4096]{2,1,0:T(8,128)(2,1)}, u32[]{:S(2)}) copy-start(bf16[1,512,4096]{2,1,0:T(8,128)(2,1)} %param.15) | copy-start | bytes 12582916
  567.7 38.4 %collective-permute-start.4 = (bf16[2,96,4096]{2,1,0:T(8,128)(2,1)S(1)}, bf16[2,96,4096]{2,1,0:T(8,128)(2,1)S(1)}, u32[]{:S(2)}, u32[]{:S(2)}) collective-permute-start(bf16[2,96,4096]{2,1,0:T(8,128)(2,1)S(1)} %fusion.39), channel_id=1, source_target_pairs={{8,0},{16,8},{24,16},{9,1},{17,9},{25,17},{10,2},{18,10},{26,18},{... | collective-permute-start | bytes 4718600 | tf_op jit(solution)/shard_map/ppermute | solution.py:22
  677.9 54.0 %collective-permute-start.5 = (bf16[2,96,4096]{2,1,0:T(8,128)(2,1)}, bf16[2,96,4096]{2,1,0:T(8,128)(2,1)}, u32[]{:S(2)}, u32[]{:S(2)}) collective-permute-start(bf16[2,96,4096]{2,1,0:T(8,128)(2,1)} %fusion.41), channel_id=1, source_target_pairs={{8,0},{16,8},{24,16},{9,1},{17,9},{25,17},{10,2},{18,10},{26,18},{... | collective-permute-start | bytes 4718600 | tf_op jit(solution)/shard_map/ppermute | solution.py:22
  689.4 77.2 %all-to-all-start = ((bf16[192,2,2048]{2,0,1:T(8,128)(2,1)}), bf16[192,2,2048]{2,0,1:T(8,128)(2,1)}, u32[]{:S(2)}, u32[]{:S(2)}) async-start(bf16[192,2,2048]{2,0,1:T(8,128)(2,1)} %copy.95), calls=%async_computation | async-start | bytes 3145728 | tf_op jit(solution)/shard_map/all_to_all | solution.py:241
  766.7 45.9 %all-to-all-start.1 = ((bf16[192,2,2048]{2,0,1:T(8,128)(2,1)}), bf16[192,2,2048]{2,0,1:T(8,128)(2,1)}, u32[]{:S(2)}, u32[]{:S(2)}) async-start(bf16[192,2,2048]{2,0,1:T(8,128)(2,1)} %fusion.63), calls=%async_computation.1 | async-start | bytes 3145728 | tf_op jit(solution)/shard_map/all_to_all | solution.py:242
  (106 other events, 646.3 us)
Sparse Core Ops, SparseCore 0:
  27.8 45.5 all-reduce.35
  124.4 45.3 all-reduce.37
  220.3 43.9 all-reduce.39
  324.0 44.3 all-reduce.41
  402.6 46.3 all-gather.8
  512.9 45.4 all-gather.10
  621.9 45.4 all-gather.12
